TPU v7x, 768 devices: a whole 4x8x12 slice. The times are simulated.
768 devices in a mesh: fsdp: 128 (over z_lo, x, y), dp: 6 (over z_hi, core).
Axes of the slice: x: 4, y: 8, z: 12 (z_hi: 3, z_lo: 4; z = z_hi * 4 + z_lo), core: 2. Of those that a mesh axis runs over, the one named last changes fastest.
Arguments:
- normed: bfloat16 [2, 98304, 4096], P(None, ('fsdp', 'dp')), may hold values from -6 to 6
- kv_cotangent: bfloat16 [2, 98304, 512], P(None, ('fsdp', 'dp')), may hold values from -6 to 6
- kv_weight: bfloat16 [4096, 512], P('fsdp'), may hold values from -0.09375 to 0.09375
- main_grad: float32 [4096, 512], P('fsdp'), may hold values from -6 to 6
- owner_order: int32 [128], replicated, may hold values from 0 to 127, each once
Outputs:
- key_rows: bfloat16 [2, 98304, 512], P(None, ('fsdp', 'dp'))
- input_grad: bfloat16 [2, 98304, 4096], P(None, ('fsdp', 'dp'))
- grad_buffer: float32 [4096, 512], P('fsdp')
Inputs may be any that keep to these rules, and one draw needn't show every extreme that they name: `owner_order`: a permutation: each value appears once.
All inputs are finite; a program needn't handle non-finite values.
Results may differ from a plain program's by a relative error of at most 0.0075.
Values may be sent and summed in bfloat16 or wider, within the bound.
A program may use at most 64 MiB of HBM per device.

v0:
```python
import math

import jax
import jax.numpy as jnp
from jax import lax
from jax.sharding import Mesh
from jax.sharding import PartitionSpec as P

FSDP = ("fsdp_0", "fsdp_1", "fsdp_2")
FSDP_DP = ("fsdp_0", "fsdp_1", "fsdp_2", "dp")


def laid_out(blocks, dim):
    blocks = jnp.moveaxis(blocks, 0, dim)
    lengths = blocks.shape
    return blocks.reshape(*lengths[:dim], lengths[dim] * lengths[dim + 1], *lengths[dim + 2 :])


def stacked_from(array, axes, order):
    blocks = array
    for k in order:
        blocks = lax.all_gather(blocks, axes[k])
    done = order[::-1]
    back = [done.index(k) for k in range(len(axes))]
    blocks = blocks.transpose(*back, *range(len(axes), blocks.ndim))
    return blocks.reshape(-1, *array.shape)


def gathered_by_axis(array, axes, order, dim):
    return laid_out(stacked_from(array, axes, order), dim)


def sum_in_order(blocks, axes, order):
    inside = blocks.shape[1:]
    blocks = blocks.reshape(*(lax.axis_size(a) for a in axes), *inside)
    blocks = jnp.moveaxis(blocks, order, range(len(axes))).reshape(-1, *inside)
    for k in order:
        blocks = lax.psum_scatter(blocks, axes[k], scatter_dimension=0, tiled=True)
    return blocks[0]


def cut_along(array, dim, devices):
    before, after = (array.shape[:dim], array.shape[dim + 1 :])
    return jnp.moveaxis(array.reshape(*before, devices, -1, *after), dim, 0)


def sum_by_axis(array, axes, order, dim):
    devices = lax.axis_size(axes)
    return sum_in_order(cut_along(array, dim, devices), axes, order)


def total_of_pieces(array, axis):
    blocks = lax.all_gather(array, axis).astype(jnp.float32)
    return blocks.sum(axis=0)


def term_from(inputs, cotangent):
    return lax.dot_general(
        inputs, cotangent, (((0,), (0,)), ((), ())), preferred_element_type=jnp.float32
    )


def body(normed, kv_cotangent, kv_weight, main_grad, owner_order):
    micro_count, tok_dev, width = normed.shape
    shard_rows, key_width = kv_weight.shape
    owners = lax.axis_size(FSDP)
    everyone = owners * lax.axis_size("dp")
    all_rows = micro_count * tok_dev
    permuted = jnp.take(normed.reshape(all_rows, owners, shard_rows), owner_order, axis=1).reshape(
        all_rows, width
    )
    flat_cot = kv_cotangent.reshape(all_rows, key_width)
    gathered = gathered_by_axis(kv_weight, FSDP, (0, 1, 2), 0)
    key_sum = jnp.dot(permuted, gathered, preferred_element_type=jnp.float32)
    grad_permuted = lax.dot_general(
        flat_cot, gathered, (((1,), (1,)), ((), ())), preferred_element_type=jnp.float32
    ).astype(jnp.bfloat16)
    indices = jnp.arange(owners, dtype=jnp.int32)
    inverse_owner = jnp.sum(
        jnp.where(owner_order[None, :] == indices[:, None], indices[None, :], 0), axis=1
    )
    input_grad = jnp.take(
        grad_permuted.reshape(all_rows, owners, shard_rows), inverse_owner, axis=1
    ).reshape(micro_count, tok_dev, width)
    shard_sum = sum_by_axis(term_from(permuted, flat_cot), FSDP, (2, 1, 0), 0)
    replica_total = total_of_pieces(shard_sum.astype(jnp.bfloat16), "dp").astype(jnp.float32)
    grad_scale = 1.0 / math.sqrt(micro_count * tok_dev * everyone)
    grad_buffer = main_grad + replica_total * grad_scale
    key_rows = key_sum.astype(jnp.bfloat16).reshape(micro_count, tok_dev, key_width)
    return (key_rows, input_grad, grad_buffer)


def solution(mesh):
    split = Mesh(
        mesh.devices.reshape(4, 4, 8, mesh.shape["dp"]), ("fsdp_0", "fsdp_1", "fsdp_2", "dp")
    )
    in_specs = (P(None, FSDP_DP, None), P(None, FSDP_DP, None), P(FSDP, None), P(FSDP, None), P())
    out_specs = (P(None, FSDP_DP, None), P(None, FSDP_DP, None), P(FSDP, None))
    return jax.shard_map(body, mesh=split, in_specs=in_specs, out_specs=out_specs, check_vma=False)
```

profile of v0, /device:TPU:1, one launch (start us, length us, event | category | flops | bytes accessed | tf_op | source)
XLA Modules:
  0.0 286.3 jit_solution(12345397831853480401)
XLA Ops:
  7.2 0.7 compare_and_fusion.1
  7.9 0.7 compare_select_fusion.1
  8.6 4.7 %copy.23 = bf16[2,128,4096]{1,0,2:T(2,128)(2,1)S(1)} copy(bf16[2,128,4096]{2,1,0:T(8,128)(2,1)} %param.7) | data formatting | bytes 4194304 | tf_op args[0]
  13.3 2.6 reshape.34
  15.9 2.3 gather_fusion
  18.2 0.3 broadcast_select_fusion
  18.5 1.2 convolution_bitcast_fusion
  19.8 0.1 copy-done.2
  19.8 4.3 %copy.26 = f32[8,4,4,32,512]{4,3,2,1,0:T(8,128)} copy(f32[8,4,4,32,512]{4,3,0,1,2:T(8,128)S(1)} %convolution_bitcast_fusion) | data formatting | bytes 16777216 | tf_op jit(solution)/shard_map/transpose | solution.py:36
  24.2 0.0 all-gather.5.cloned.1.call-start
  24.2 0.7 copy-done.4
  24.9 13.7 %all-gather = bf16[128,512]{1,0:T(8,128)(2,1)S(1)} all-gather(bf16[32,512]{1,0:T(8,128)(2,1)S(1)} %copy-done.4), channel_id=2, replica_groups=mesh['fsdp_0'=4,'fsdp_1'=4,'fsdp_2'=8,'dp'=6] {'fsdp_0'}, dimensions={0}, use_global_device_ids=true | all-gather | bytes 163840 | tf_op jit(solution)/shard_map/all_gather | solution.py:22
  38.6 11.4 %all-gather.1 = bf16[16,32,512]{2,1,0:T(8,128)(2,1)} all-gather(bf16[4,32,512]{2,1,0:T(8,128)(2,1)S(1)} %bitcast.45), channel_id=3, replica_groups=mesh['fsdp_0'=4,'fsdp_1'=4,'fsdp_2'=8,'dp'=6] {'fsdp_1'}, dimensions={0}, use_global_device_ids=true | all-gather | bytes 655360 | tf_op jit(solution)/shard_map/all_gather | solution.py:22
  50.0 0.0 reduce-scatter.6.cloned.1.call-start
  50.1 81.7 %reduce-scatter.4.cloned.1.call-done = f32[16,32,512]{2,1,0:T(8,128)} async-done(((f32[128,32,512]{2,1,0:T(8,128)}), f32[16,32,512]{2,1,0:T(8,128)}) %reduce-scatter.4.cloned.1.call-update) | async-done | bytes 1048592 | tf_op jit(solution)/shard_map/reduce_scatter | solution.py:38
  131.8 0.0 reduce-scatter.8.cloned.1.call-start
  131.9 0.1 select_reduce_fusion
  132.0 61.0 %all-gather.5.cloned.1.call-done = bf16[32,4,32,512]{3,2,1,0:T(8,128)(2,1)} async-done(((bf16[4,4,32,512]{3,2,1,0:T(8,128)(2,1)}), bf16[32,4,32,512]{3,2,1,0:T(8,128)(2,1)}) %all-gather.5.cloned.1.call-update) | async-done | bytes 4194320 | tf_op jit(solution)/shard_map/all_gather | solution.py:22
  193.0 2.7 copy.24
  195.6 1.9 copy-done.1
  197.6 1.3 convolution_convert_fusion
  198.9 2.5 copy.25
  201.3 2.3 gather_fusion.1
  203.6 22.1 %reduce-scatter.6.cloned.1.call-done = f32[4,32,512]{2,1,0:T(8,128)} async-done(((f32[16,32,512]{2,1,0:T(8,128)}), f32[4,32,512]{2,1,0:T(8,128)}) %reduce-scatter.6.cloned.1.call-update) | async-done | bytes 262160 | tf_op jit(solution)/shard_map/reduce_scatter | solution.py:38
  225.7 1.6 select_bitcast_fusion
  227.3 2.5 reshape.39
  229.9 3.8 %copy.27 = bf16[2,128,4096]{2,1,0:T(8,128)(2,1)} copy(bf16[2,128,4096]{1,0,2:T(2,128)(2,1)S(1)} %reshape.39) | data formatting | bytes 4194304
  233.6 4.8 %convolution_convert_fusion.1 = bf16[256,512]{1,0:T(8,128)(2,1)} fusion(bf16[256,4096]{0,1:T(8,128)(2,1)} %bitcast.42, bf16[4096,512]{1,0:T(8,128)(2,1)} %bitcast.40), kind=kOutput, calls=%fused_computation.6 | convolution fusion | flops 1073872896 | bytes 6553600 | tf_op jit(solution)/shard_map/dot_general | solution.py:74
  238.4 20.2 %reduce-scatter.8.cloned.1.call-done = f32[1,32,512]{2,1,0:T(8,128)} async-done(((f32[4,32,512]{2,1,0:T(8,128)}), f32[1,32,512]{2,1,0:T(8,128)}) %reduce-scatter.8.cloned.1.call-update) | async-done | bytes 65552 | tf_op jit(solution)/shard_map/reduce_scatter | solution.py:38
  258.6 0.8 convert_element_type.15
  259.5 19.6 %all_gather.28 = bf16[6,32,512]{2,1,0:T(8,128)(2,1)S(1)} all-gather(bf16[1,32,512]{2,1,0:T(8,128)(2,1)S(1)} %convert_element_type.15), channel_id=1, replica_groups=mesh['fsdp_0'=4,'fsdp_1'=4,'fsdp_2'=8,'dp'=6] {'dp'}, dimensions={0}, use_global_device_ids=true | all-gather | bytes 229376 | tf_op jit(solution)/shard_map/all_gather | solution.py:53
  279.1 0.6 multiply_add_fusion
  (19 shorter events, 0.2 us)
Async XLA Ops:
  7.2 11.3 %copy-start = (bf16[2,128,512]{2,1,0:T(8,128)(2,1)S(1)}, bf16[2,128,512]{2,1,0:T(8,128)(2,1)}, u32[]{:S(2)}) copy-start(bf16[2,128,512]{2,1,0:T(8,128)(2,1)} %param.8) | copy-start | bytes 786436
  7.2 124.6 %reduce-scatter.4.cloned.1.call-start = ((), (), s32[]{:S(2)}) async-start(), calls=%async_computation.3 | async-start | bytes 9437184 | tf_op jit(solution)/shard_map/reduce_scatter | solution.py:38
  18.5 1.3 copy-start.2
  24.1 0.8 copy-start.4
  24.1 107.7 %copy-start.5 = (s32[128]{0:T(128)S(1)}, s32[128]{0:T(128)}, u32[]{:S(2)}) copy-start(s32[128]{0:T(128)} %param.11) | copy-start | bytes 1540
  24.2 168.8 %all-gather.5.cloned.1.call-start = ((), (), s32[]{:S(2)}) async-start(), calls=%async_computation.6 | async-start | bytes 4718592 | tf_op jit(solution)/shard_map/all_gather | solution.py:22
  50.0 175.7 %reduce-scatter.6.cloned.1.call-start = ((), (), s32[]{:S(2)}) async-start(), calls=%async_computation.4 | async-start | bytes 1310720 | tf_op jit(solution)/shard_map/reduce_scatter | solution.py:38
  131.8 126.8 %reduce-scatter.8.cloned.1.call-start = ((), (), s32[]{:S(2)}) async-start(), calls=%async_computation.5 | async-start | bytes 327680 | tf_op jit(solution)/shard_map/reduce_scatter | solution.py:38
  195.6 1.9 copy-start.1
  233.6 45.5 %copy-start.3 = (f32[32,512]{1,0:T(8,128)S(1)}, f32[32,512]{1,0:T(8,128)}, u32[]{:S(2)}) copy-start(f32[32,512]{1,0:T(8,128)} %param.10) | copy-start | bytes 196612
Sparse Core Ops, SparseCore 0:
  24.3 107.4 reduce-scatter.3
  134.1 58.7 all-gather.4
  196.1 29.5 reduce-scatter.5
  228.6 29.9 reduce-scatter.7
where the time goes:
time: 287 us; the launch traced here: 286 us
  waiting for transfers between devices  185 us (64%)
  blocking collectives  44.7 us (16%)
  local copies, waits for them, and re-layouts  30.3 us (11%)
  between operations  13.9 us (5%)
  matrix products  7.35 us (3%)
  other arithmetic  4.86 us (2%)
    reduce_scatter x3, waiting for transfers between devices, sum_in_order(): blocks = lax.psum_scatter(blocks, axes[k], scatter_dimension=0, tiled=True)  124 us
    all_gather x1, waiting for transfers between devices, stacked_from(): blocks = lax.all_gather(blocks, axes[k])  61 us
    all_gather x2, blocking collectives, stacked_from(): blocks = lax.all_gather(blocks, axes[k])  25.1 us
    all_gather x1, blocking collectives, total_of_pieces(): blocks = lax.all_gather(array, axis).astype(jnp.float32)  19.6 us
    unnamed x14, local copies, waits for them, and re-layouts  11.2 us
  transfers between devices with their start and end apart: 4, of which 4 were waited for; matrix products, arithmetic and copies ran while one was open for 8% of the time, Pallas kernels for 0%

commit v1 on v0

v1 whole, which is shorter than its diff:
```python
import functools
import math

import jax
import jax.numpy as jnp
from jax import lax
from jax.experimental import pallas as pl
from jax.experimental.pallas import tpu as pltpu
from jax.sharding import Mesh
from jax.sharding import PartitionSpec as P

MESH = pl.DeviceIdType.MESH
NAMES = ("zl", "x", "y", "zh", "core")
F32, BF16 = jnp.float32, jnp.bfloat16
CHUNK = 512
PLUS, MINUS = 0, 1


def kernel(
    ny, nh, scale,
    order, inv, normed, cot, weight, main, key_out, ig_out, gb_out,
    nv, cv, mv, grad, gw, ow, wv, igv, kacc, kv,
    snd, rcv, sq, tq, mq, r1, sp, tp, mp, r2, sy, yb, sh, hb, fb,
    loc, ays, ayr, aps, apr, aqs, aqr, ads, adr,
    rds, rdr, rqs, rqr, rps, rpr, rys, ryr, rhs, rhr, fin, out,
):
    half = ny // 2
    micro, tok, width = normed.shape
    rows, hw = gw.shape[1:]
    blocks_in_chunk = CHUNK // rows
    a, x, y = lax.axis_index("zl"), lax.axis_index("x"), lax.axis_index("y")
    h, c = lax.axis_index("zh"), lax.axis_index("core")
    nz = 4 * nh
    z = h * 4 + a

    def z_of(d):
        to = lax.rem(z + d + nz, nz)
        return lax.rem(to, 4), lax.div(to, 4)

    def heavy(d):
        az, hz = z_of(d)
        xx = lax.rem(x + d + 4, 4)
        return (a + (1 - c) * (az - a), x + c * (xx - x), y, h + (1 - c) * (hz - h), c)

    def light(d):
        az, hz = z_of(d)
        xx = lax.rem(x + d + 4, 4)
        return (a + c * (az - a), x + (1 - c) * (xx - x), y, h + c * (hz - h), c)

    q = a + c * (x - a)
    p = x + c * (a - x)
    partner = (a, x, y, h, 1 - c)
    heavies = (heavy(1), heavy(-1))
    lights = (light(1), light(-1))
    y_peers = [(a, x, lax.rem(y + d, ny), h, c) for d in range(1, ny)]
    h_peers = [(a, x, y, lax.rem(h + d, nh), c) for d in range(1, nh)]
    peers = [partner, *heavies, *lights, *y_peers, *h_peers]

    def rel(v, d):
        return lax.rem(v + d, 4)

    def slots(qq, pp):
        return (qq * 4 + pp) * ny

    def owner(cc, qq, pp):
        return ((qq + cc * (pp - qq)) * 4 + (pp + cc * (qq - pp))) * ny

    def remote(src, dst, s, r, to):
        return pltpu.make_async_remote_copy(
            src_ref=src, dst_ref=dst, send_sem=s, recv_sem=r, device_id=to, device_id_type=MESH
        )

    loads = [pltpu.make_async_copy(normed.at[m], nv.at[pl.ds(m * tok, tok)], loc.at[m]) for m in range(micro)]
    loads += [
        pltpu.make_async_copy(cot.at[m], cv.at[pl.ds(m * tok, tok)], loc.at[micro + m]) for m in range(micro)
    ]
    mine = slots(q, p) + y
    load_w = pltpu.make_async_copy(
        weight.at[:, pl.ds(pl.multiple_of(c * hw, hw), hw)], gw.at[mine], loc.at[2 * micro]
    )
    load_m = [
        pltpu.make_async_copy(main.at[:, pl.ds(k * hw, hw)], mv.at[k], loc.at[2 * micro + 1 + k]) for k in range(2)
    ]
    load_w.start()
    for copy in loads + load_m:
        copy.start()

    barrier = pltpu.get_barrier_semaphore()
    for peer in peers:
        pl.semaphore_signal(barrier, inc=1, device_id=peer, device_id_type=MESH)

    for copy in loads:
        copy.wait()

    def grad_chunk(i, carry):
        at = pl.multiple_of(i * CHUNK, CHUNK)
        d = lax.dot_general(
            nv[:, pl.ds(at, CHUNK)], cv[...], (((0,), (0,)), ((), ())), preferred_element_type=F32
        )
        first = i * blocks_in_chunk
        grad[0, pl.ds(first, blocks_in_chunk)] = d[:, :hw].reshape(blocks_in_chunk, rows, hw)
        grad[1, pl.ds(first, blocks_in_chunk)] = d[:, hw:].reshape(blocks_in_chunk, rows, hw)
        return carry

    lax.fori_loop(0, width // CHUNK, grad_chunk, 0)

    pl.semaphore_wait(barrier, len(peers))
    load_w.wait()
    ag_y = [
        remote(gw.at[mine], gw.at[mine], ays.at[d], ayr.at[d], y_peers[d]) for d in range(ny - 1)
    ]
    for copy in ag_y:
        copy.start()

    sent = list(ag_y)

    def send(copy):
        copy.start()
        sent.append(copy)
        return copy

    rs_d = {}
    for dq in (2, 1, 3, 0):
        for dp in (0, 1, 2, 3) if dq == 2 else (2, 1, 3, 0):
            qq, pp = rel(p, dq), rel(q, dp)
            st, base = slots(qq, pp), owner(1 - c, qq, pp)

            def convert(i, carry, st=st, base=base):
                snd[st + i] = grad[1 - c, order[base + i]].astype(BF16)
                return carry

            lax.fori_loop(0, ny, convert, 0, unroll=4)
            k = dq * 4 + dp
            rs_d[dq, dp] = send(
                remote(snd.at[pl.ds(st, ny)], rcv.at[pl.ds(st, ny)], rds.at[k], rdr.at[k], partner)
            )

    def summed(dq, dp, store, extra=()):
        qq, pp = rel(q, dq), rel(p, dp)
        st, base = slots(qq, pp), owner(c, qq, pp)

        def step(i, carry):
            v = grad[c, order[base + i]] + rcv[st + i].astype(F32)
            for ref in extra:
                v += ref[i].astype(F32)
            store(st, i, v)
            return carry

        lax.fori_loop(0, ny, step, 0, unroll=4)
        return st

    def to_sq(st, i, v):
        sq[st + i] = v.astype(BF16)

    two_away = {PLUS: (0, 2), MINUS: (1, 3)}

    rs_t = {}
    for k in range(2):
        for way in (PLUS, MINUS):
            dp = two_away[way][k]
            rs_d[2, dp].wait_recv()
            st = summed(2, dp, to_sq)
            rs_t[way, k] = send(
                remote(sq.at[pl.ds(st, ny)], tq.at[way, k], rqs.at[way, 4 + k], rqr.at[way, 4 + k], heavies[way])
            )

    rs_m = {}

    def rs_main(way, dp, extra=()):
        dq = 1 if way == PLUS else 3
        rs_d[dq, dp].wait_recv()
        st = summed(dq, dp, to_sq, extra)
        rs_m[way, dp] = send(
            remote(sq.at[pl.ds(st, ny)], mq.at[way, dp], rqs.at[way, dp], rqr.at[way, dp], heavies[way])
        )

    rs_main(MINUS, 2)
    rs_main(PLUS, 1)
    rs_main(PLUS, 3)
    rs_main(MINUS, 0)

    for copy in ag_y:
        copy.wait_recv()
    ag_p, ag_q, ag_d = {}, {}, {}

    def piece(dq, dp):
        return gw.at[pl.ds(slots(rel(q, dq), rel(p, dp)), ny)]

    def half_piece(dq, dp, j):
        return gw.at[pl.ds(slots(rel(q, dq), rel(p, dp)) + j * half, half)]

    def ag_light(way, dp, j, k):
        ag_p[way, k] = send(
            remote(half_piece(0, dp, j), half_piece(0, dp, j), aps.at[way, k], apr.at[way, k], lights[way])
        )

    def ag_heavy(way, dq, dp, k):
        ag_q[way, k] = send(remote(piece(dq, dp), piece(dq, dp), aqs.at[way, k], aqr.at[way, k], heavies[way]))

    def ag_across(dq, dp):
        st = slots(rel(q, dq), rel(p, dp))
        k = dq * 4 + dp
        ag_d[k] = send(remote(gw.at[pl.ds(st, ny)], ow.at[pl.ds(st, ny)], ads.at[k], adr.at[k], partner))

    ag_light(PLUS, 0, 0, 0)
    ag_light(MINUS, 0, 1, 1)
    ag_light(PLUS, 0, 1, 1)
    ag_light(MINUS, 0, 0, 0)

    for k in (1, 0):
        rs_t[PLUS, k].wait_recv()
        rs_main(PLUS, two_away[PLUS][k], (tq.at[PLUS, k],))
        rs_t[MINUS, k].wait_recv()
        rs_main(MINUS, two_away[MINUS][k], (tq.at[MINUS, k],))

    def ag_own(dp):
        ag_heavy(PLUS, 0, dp, dp)
        ag_heavy(MINUS, 0, dp, dp)
        ag_across(0, dp)

    ag_own(0)
    ag_p[PLUS, 0].wait_recv()
    ag_light(PLUS, 3, 0, 2)
    ag_p[MINUS, 1].wait_recv()
    ag_light(MINUS, 1, 1, 2)
    ag_p[PLUS, 1].wait_recv()
    ag_own(3)
    ag_p[MINUS, 0].wait_recv()
    ag_own(1)
    ag_p[PLUS, 2].wait_recv()
    ag_p[MINUS, 2].wait_recv()
    ag_own(2)

    def heavy_sum(dp):
        rs_d[0, dp].wait_recv()
        rs_m[PLUS, dp].wait_recv()
        rs_m[MINUS, dp].wait_recv()

        def store(st, i, v):
            r1[dp, i] = v

        summed(0, dp, store, (mq.at[PLUS, dp], mq.at[MINUS, dp]))

    rs_pt, rs_pm = {}, {}

    def light_send(way, dp, j, dst, k, table, extra=None):
        def step(i, carry):
            v = r1[dp, j * half + i]
            if extra is not None:
                v += extra[i].astype(F32)
            sp[dp, j * half + i] = v.astype(BF16)
            return carry

        lax.fori_loop(0, half, step, 0, unroll=True)
        table[way, j] = send(
            remote(sp.at[dp, pl.ds(j * half, half)], dst, rps.at[way, k], rpr.at[way, k], lights[way])
        )

    heavy_sum(2)
    light_send(PLUS, 2, 0, tp.at[PLUS], 2, rs_pt)
    light_send(MINUS, 2, 1, tp.at[MINUS], 2, rs_pt)
    heavy_sum(1)
    light_send(PLUS, 1, 1, mp.at[PLUS, pl.ds(half, half)], 1, rs_pm)
    heavy_sum(3)
    light_send(MINUS, 3, 0, mp.at[MINUS, pl.ds(0, half)], 0, rs_pm)
    heavy_sum(0)

    forwards = {PLUS: (0, 1), MINUS: (3, 2)}

    def ag_arrived(way, dp):
        ag_q[way, dp].wait_recv()
        dq = 3 if way == PLUS else 1
        if dp in forwards[way]:
            ag_heavy(way, dq, dp, 4 + forwards[way].index(dp))
        ag_across(dq, dp)

    ag_arrived(PLUS, 0)
    ag_arrived(MINUS, 0)
    ag_arrived(PLUS, 3)
    ag_arrived(MINUS, 3)

    rs_pt[PLUS, 0].wait_recv()
    light_send(PLUS, 1, 0, mp.at[PLUS, pl.ds(0, half)], 0, rs_pm, tp.at[PLUS])
    rs_pt[MINUS, 1].wait_recv()
    light_send(MINUS, 3, 1, mp.at[MINUS, pl.ds(half, half)], 1, rs_pm, tp.at[MINUS])

    ag_arrived(PLUS, 1)
    ag_arrived(MINUS, 1)
    ag_arrived(PLUS, 2)
    ag_arrived(MINUS, 2)

    for copy in rs_pm.values():
        copy.wait_recv()

    def light_sum(i, carry):
        v = r1[0, i] + mp[PLUS, i].astype(F32) + mp[MINUS, i].astype(F32)
        r2[i] = v
        sy[i] = v.astype(BF16)
        return carry

    lax.fori_loop(0, ny, light_sum, 0, unroll=4)
    rs_y = [
        send(remote(sy.at[lax.rem(y + d + 1, ny)], yb.at[d], rys.at[d], ryr.at[d], y_peers[d]))
        for d in range(ny - 1)
    ]

    for way in (PLUS, MINUS):
        for k in range(2):
            ag_q[way, 4 + k].wait_recv()
            ag_across(2, forwards[way][k])

    for copy in rs_y:
        copy.wait_recv()
    total = r2[y]
    for d in range(ny - 1):
        total += yb[d].astype(F32)
    rounded = total.astype(BF16)
    sh[...] = rounded
    hb[h] = rounded
    rs_h = [send(remote(sh, hb.at[h], rhs.at[d], rhr.at[d], h_peers[d])) for d in range(nh - 1)]

    for copy in ag_d.values():
        copy.wait_recv()

    def place(o, carry):
        f = inv[o]
        swapped = lax.rem(f, ny) + (lax.rem(lax.div(f, ny), 4) * 4 + lax.div(f, 4 * ny)) * ny
        at = pl.ds(pl.multiple_of(o * rows, rows), rows)
        wv[c, at] = gw[f + c * (swapped - f)]
        wv[1 - c, at] = ow[f + (1 - c) * (swapped - f)]
        return carry

    lax.fori_loop(0, gw.shape[0], place, 0, unroll=4)

    kacc[...] = jnp.zeros_like(kacc)

    def product(i, carry):
        at = pl.ds(pl.multiple_of(i * CHUNK, CHUNK), CHUNK)
        w0, w1 = wv[0, at], wv[1, at]
        n = nv[:, at]
        kacc[0] += jnp.dot(n, w0, preferred_element_type=F32)
        kacc[1] += jnp.dot(n, w1, preferred_element_type=F32)
        contract = (((1,), (1,)), ((), ()))
        g = lax.dot_general(cv[:, :hw], w0, contract, preferred_element_type=F32)
        g += lax.dot_general(cv[:, hw:], w1, contract, preferred_element_type=F32)
        igv[:, at] = g.astype(BF16)
        return carry

    lax.fori_loop(0, width // CHUNK, product, 0)
    kv[:, :hw] = kacc[0].astype(BF16)
    kv[:, hw:] = kacc[1].astype(BF16)
    stores = [pltpu.make_async_copy(igv.at[pl.ds(m * tok, tok)], ig_out.at[m], out.at[m]) for m in range(micro)]
    stores += [
        pltpu.make_async_copy(kv.at[pl.ds(m * tok, tok)], key_out.at[m], out.at[micro + m]) for m in range(micro)
    ]
    for copy in stores:
        copy.start()

    for copy in rs_h:
        copy.wait_recv()
    for copy in load_m:
        copy.wait()
    total = hb[0].astype(F32)
    for k in range(1, nh):
        total += hb[k].astype(F32)
    fb[c] = mv[c] + total * scale
    last = send(remote(fb.at[c], fb.at[c], fin.at[0], fin.at[1], partner))
    last.wait_recv()
    for k in range(2):
        stores.append(pltpu.make_async_copy(fb.at[k], gb_out.at[:, pl.ds(k * hw, hw)], out.at[2 * micro + k]))
        stores[-1].start()
    for copy in sent:
        copy.wait_send()
    for copy in stores:
        copy.wait()


def body(ny, nh, normed, kv_cotangent, kv_weight, main_grad, owner_order):
    micro, tok, width = normed.shape
    rows, key_width = kv_weight.shape
    owners = 16 * ny
    hw = key_width // 2
    half = ny // 2
    everyone = owners * nh * 2
    scale = 1.0 / math.sqrt(micro * tok * everyone)
    indices = jnp.arange(owners, dtype=jnp.int32)
    inv = jnp.sum(jnp.where(owner_order[None, :] == indices[:, None], indices[None, :], 0), axis=1)
    dma = pltpu.SemaphoreType.DMA
    anywhere = pl.BlockSpec(memory_space=pl.ANY)
    scalars = pl.BlockSpec(memory_space=pltpu.SMEM)
    block = (rows, hw)
    return pl.pallas_call(
        functools.partial(kernel, ny, nh, scale),
        out_shape=(
            jax.ShapeDtypeStruct((micro, tok, key_width), BF16),
            jax.ShapeDtypeStruct((micro, tok, width), BF16),
            jax.ShapeDtypeStruct((rows, key_width), F32),
        ),
        in_specs=[scalars, scalars] + [anywhere] * 4,
        out_specs=(anywhere,) * 3,
        scratch_shapes=[
            pltpu.VMEM((micro * tok, width), BF16),
            pltpu.VMEM((micro * tok, key_width), BF16),
            pltpu.VMEM((2, *block), F32),
            pltpu.VMEM((2, owners, *block), F32),
            pltpu.VMEM((owners, *block), BF16),
            pltpu.VMEM((owners, *block), BF16),
            pltpu.VMEM((2, width, hw), BF16),
            pltpu.VMEM((micro * tok, width), BF16),
            pltpu.VMEM((2, micro * tok, hw), F32),
            pltpu.VMEM((micro * tok, key_width), BF16),
            pltpu.VMEM((owners, *block), BF16),
            pltpu.VMEM((owners, *block), BF16),
            pltpu.VMEM((owners, *block), BF16),
            pltpu.VMEM((2, 2, ny, *block), BF16),
            pltpu.VMEM((2, 4, ny, *block), BF16),
            pltpu.VMEM((4, ny, *block), F32),
            pltpu.VMEM((4, ny, *block), BF16),
            pltpu.VMEM((2, half, *block), BF16),
            pltpu.VMEM((2, ny, *block), BF16),
            pltpu.VMEM((ny, *block), F32),
            pltpu.VMEM((ny, *block), BF16),
            pltpu.VMEM((ny - 1, *block), BF16),
            pltpu.VMEM(block, BF16),
            pltpu.VMEM((nh, *block), BF16),
            pltpu.VMEM((2, *block), F32),
            dma((2 * micro + 3,)),
            dma((ny - 1,)),
            dma((ny - 1,)),
            dma((2, 3)),
            dma((2, 3)),
            dma((2, 6)),
            dma((2, 6)),
            dma((16,)),
            dma((16,)),
            dma((16,)),
            dma((16,)),
            dma((2, 6)),
            dma((2, 6)),
            dma((2, 3)),
            dma((2, 3)),
            dma((ny - 1,)),
            dma((ny - 1,)),
            dma((max(nh - 1, 1),)),
            dma((max(nh - 1, 1),)),
            dma((2,)),
            dma((2 * micro + 2,)),
        ],
        compiler_params=pltpu.CompilerParams(
            collective_id=0, has_side_effects=True, vmem_limit_bytes=60 * 1024 * 1024
        ),
    )(owner_order, inv, normed, kv_cotangent, kv_weight, main_grad)


def solution(mesh):
    owners = mesh.shape["fsdp"]
    ny, nh = owners // 16, mesh.shape["dp"] // 2
    split = Mesh(mesh.devices.reshape(4, 4, ny, nh, 2), NAMES)
    tokens, fsdp = P(None, NAMES, None), P(NAMES[:3], None)
    return jax.shard_map(
        functools.partial(body, ny, nh),
        mesh=split,
        in_specs=(tokens, tokens, fsdp, fsdp, P()),
        out_specs=(tokens, tokens, fsdp),
        check_vma=False,
    )
```

time: 287 us -> 66.7 us (0.23)
  waiting for transfers between devices: 185 us -> 0 us
  Pallas kernels: 0 us -> 59.1 us
  blocking collectives: 44.7 us -> 0 us
  local copies, waits for them, and re-layouts: 30.3 us -> 5.46 us
  between operations: 13.9 us -> 0.64 us
  matrix products: 7.35 us -> 0 us
  other arithmetic: 4.86 us -> 1.28 us
    reduce_scatter x3 -> x0, waiting for transfers between devices: 124 us -> none  [sum_in_order(): blocks = lax.psum_scatter(blocks, axes[k], scatter_dimension=0, tiled=True)]
    all_gather x1 -> x0, waiting for transfers between devices: 61 us -> none  [stacked_from(): blocks = lax.all_gather(blocks, axes[k])]
    pallas_call x0 -> x1, Pallas kernels: none -> 59.1 us  [body(): pl.pallas_call(functools.partial(kernel, ny, nh, scale), out_shape=(jax.S...]
    all_gather x3 -> x0, blocking collectives: 44.7 us -> none  [the longest x2 25.1 us: stacked_from(): blocks = lax.all_gather(blocks, axes[k])]
    dot_general x3 -> x0, matrix products: 7.35 us -> none  [the longest x1 4.82 us: body(): key_sum = jnp.dot(permuted, gathered, preferred_element_type=jnp.float32)]
    transpose x2 -> x0, local copies, waits for them, and re-layouts: 6.96 us -> none  [the longest x1 4.3 us: sum_in_order(): blocks = jnp.moveaxis(blocks, order, range(len(axes))).reshape(-1, *inside)]
    unnamed x14 -> x5, local copies, waits for them, and re-layouts: 11.2 us -> 5.46 us
    reshape x2 -> x0, local copies, waits for them, and re-layouts: 5.16 us -> none  [the longest x1 2.61 us: body(): normed.reshape(all_rows, owners, shard_rows)]
  transfers between devices with their start and end apart: 4 -> 0, of which waited for: 4 -> 0; matrix products, arithmetic and copies ran while one was open for 8% -> 0% of each run, Pallas kernels for 0% -> 0%
where the time goes in v1:
time: 66.7 us; the launch traced here: 66.5 us
  Pallas kernels  59.1 us (89%)
  local copies, waits for them, and re-layouts  5.46 us (8%)
  other arithmetic  1.28 us (2%)
    pallas_call x1, Pallas kernels, body(): pl.pallas_call(functools.partial(kernel, ny, nh, scale), out_shape=(jax.S...  59.1 us
    unnamed x5, local copies, waits for them, and re-layouts  5.46 us

profile of v1, /device:TPU:1, one launch (start us, length us, event | category | flops | bytes accessed | tf_op | source)
XLA Modules:
  0.0 66.5 jit_solution(6488885072959853250)
XLA Ops:
  0.6 1.3 %select_reduce_fusion.inv = s32[128]{0:T(128)} fusion(s32[128]{0:T(128)} %order.1), kind=kLoop, calls=%fused_computation | loop fusion | flops 49024 | bytes 1024 | tf_op jit(solution)/shard_map/reduce_sum | solution.py:387
  1.9 59.1 %shard_map.76 = (bf16[2,128,512]{2,1,0:T(8,128)(2,1)}, bf16[2,128,4096]{2,1,0:T(8,128)(2,1)}, f32[32,512]{1,0:T(8,128)}) custom-call(s32[128]{0:T(128)} %order.1, s32[128]{0:T(128)} %select_reduce_fusion.inv, bf16[2,128,4096]{2,1,0:T(8,128)(2,1)} %normed.1, bf16[2,128,512]{2,1,0:T(8,128)(2,1)} %cot.1, bf16[32,512]{1,0:T(8,128)(2,1)} %weight.1, f32[32,512]{1,0:T(8,128)} %main.1), custom_call_target="tpu_custom_call" | custom-call | tf_op jit(solution)/shard_map/pallas_call | solution.py:392
  61.0 1.7 %copy.11 = bf16[2,128,512]{2,1,0:T(8,128)(2,1)} copy(bf16[2,128,512]{2,1,0:T(8,128)(2,1)} %get-tuple-element.6) | data formatting | bytes 524288
  62.7 0.0 copy-start
  62.7 3.2 %copy.12 = bf16[2,128,4096]{2,1,0:T(8,128)(2,1)} copy(bf16[2,128,4096]{2,1,0:T(8,128)(2,1)} %get-tuple-element.7) | data formatting | bytes 4194304
  65.8 0.0 copy-done
  65.8 0.6 copy.13
Async XLA Ops:
  62.7 3.2 %copy-start = (f32[32,512]{1,0:T(8,128)S(1)}, f32[32,512]{1,0:T(8,128)}, u32[]{:S(2)}) copy-start(f32[32,512]{1,0:T(8,128)} %get-tuple-element.8) | copy-start | bytes 196612

commit v2 on v1

v2 whole, which is shorter than its diff:
```python
import functools
import math

import jax
import jax.numpy as jnp
from jax import lax
from jax.experimental import pallas as pl
from jax.experimental.pallas import tpu as pltpu
from jax.sharding import Mesh
from jax.sharding import PartitionSpec as P

MESH = pl.DeviceIdType.MESH
NAMES = ("zl", "x", "y", "zh", "core")
F32, BF16 = jnp.float32, jnp.bfloat16
CHUNK = 512
PLUS, MINUS = 0, 1


def kernel(
    ny, nh, scale,
    order_in, normed, cot, weight, main, key_out, ig_out, gb_out,
    order, inv, inv_row, nv, cv, mv, grad, gow, kacc,
    snd, rcv, sq, tq, mq, r1, sp, tp, mp, r2, sy, yb, sh, hb, fb,
    loc, out, ayr, apr, aqr, adr, rdr, rqr, rpr, ryr, rhr, fin,
):
    half = ny // 2
    micro, tok, width = normed.shape
    owners, rows, hw = gow.shape[1:]
    blocks_in_chunk = CHUNK // rows
    a, x, y = lax.axis_index("zl"), lax.axis_index("x"), lax.axis_index("y")
    h, c = lax.axis_index("zh"), lax.axis_index("core")
    nz = 4 * nh
    gw, ow = gow.at[c], gow.at[1 - c]
    z = h * 4 + a

    def z_of(d):
        to = lax.rem(z + d + nz, nz)
        return lax.rem(to, 4), lax.div(to, 4)

    def heavy(d):
        az, hz = z_of(d)
        xx = lax.rem(x + d + 4, 4)
        return (a + (1 - c) * (az - a), x + c * (xx - x), y, h + (1 - c) * (hz - h), c)

    def light(d):
        az, hz = z_of(d)
        xx = lax.rem(x + d + 4, 4)
        return (a + c * (az - a), x + (1 - c) * (xx - x), y, h + c * (hz - h), c)

    q = a + c * (x - a)
    p = x + c * (a - x)
    partner = (a, x, y, h, 1 - c)
    heavies = (heavy(1), heavy(-1))
    lights = (light(1), light(-1))
    y_peers = [(a, x, lax.rem(y + d, ny), h, c) for d in range(1, ny)]
    h_peers = [(a, x, y, lax.rem(h + d, nh), c) for d in range(1, nh)]
    peers = [partner, *heavies, *lights, *y_peers, *h_peers]

    def rel(v, d):
        return lax.rem(v + d, 4)

    def slots(qq, pp):
        return (qq * 4 + pp) * ny

    def owner(cc, qq, pp):
        return ((qq + cc * (pp - qq)) * 4 + (pp + cc * (qq - pp))) * ny

    def remote(src, dst, s, r, to):
        return pltpu.make_async_remote_copy(
            src_ref=src, dst_ref=dst, send_sem=s, recv_sem=r, device_id=to, device_id_type=MESH
        )

    mine = slots(q, p) + y
    load_w = pltpu.make_async_copy(
        weight.at[:, pl.ds(pl.multiple_of(c * hw, hw), hw)], gow.at[c, mine], loc.at[0]
    )
    load_order = pltpu.make_async_copy(order_in, order, loc.at[1])
    loads = [
        pltpu.make_async_copy(cot.at[m], cv.at[pl.ds(m * tok, tok)], loc.at[2 + m]) for m in range(micro)
    ]
    wide = width // 2
    loads_n = [
        [
            pltpu.make_async_copy(
                normed.at[m, :, pl.ds(k * wide, wide)],
                nv.at[pl.ds(m * tok, tok), pl.ds(k * wide, wide)],
                loc.at[2 + (k + 1) * micro + m],
            )
            for m in range(micro)
        ]
        for k in range(2)
    ]
    load_m = [
        pltpu.make_async_copy(main.at[:, pl.ds(k * hw, hw)], mv.at[k], loc.at[2 + 3 * micro + k]) for k in range(2)
    ]
    load_w.start()
    for copy in loads + loads_n[0] + loads_n[1] + [load_order] + load_m:
        copy.start()

    barrier = pltpu.get_barrier_semaphore()
    for peer in peers:
        pl.semaphore_signal(barrier, inc=1, device_id=peer, device_id_type=MESH)

    def grad_chunk(i, carry):
        at = pl.multiple_of(i * CHUNK, CHUNK)
        d = lax.dot_general(
            nv[:, pl.ds(at, CHUNK)], cv[...], (((0,), (0,)), ((), ())), preferred_element_type=F32
        )
        first = i * blocks_in_chunk
        grad[0, pl.ds(first, blocks_in_chunk)] = d[:, :hw].reshape(blocks_in_chunk, rows, hw)
        grad[1, pl.ds(first, blocks_in_chunk)] = d[:, hw:].reshape(blocks_in_chunk, rows, hw)
        return carry

    chunks = width // CHUNK
    sent = []

    def send(copy, group, size):
        copy.start()
        sent.append((group, size))
        return copy

    for copy in loads + loads_n[0]:
        copy.wait()
    lax.fori_loop(0, chunks // 2, grad_chunk, 0)
    load_w.wait()
    pl.semaphore_wait(barrier, len(peers))
    ag_y = [
        send(remote(gow.at[c, mine], gow.at[c, mine], out.at[0], ayr.at[0], y_peers[d]), 0, 1)
        for d in range(ny - 1)
    ]
    for copy in loads_n[1]:
        copy.wait()
    lax.fori_loop(chunks // 2, chunks, grad_chunk, 0)
    load_order.wait()

    rs_d = {}
    for dq in (2, 1, 3, 0):
        for dp in (0, 1, 2, 3) if dq == 2 else (2, 1, 3, 0):
            qq, pp = rel(p, dq), rel(q, dp)
            st, base = slots(qq, pp), owner(1 - c, qq, pp)

            def convert(i, carry, st=st, base=base):
                snd[st + i] = grad[1 - c, order[0, base + i]].astype(BF16)
                return carry

            lax.fori_loop(0, ny, convert, 0, unroll=4)
            rs_d[dq, dp] = send(
                remote(snd.at[pl.ds(st, ny)], rcv.at[pl.ds(st, ny)], out.at[1], rdr.at[dq * 4 + dp], partner), 1, ny
            )

    def summed(dq, dp, store, extra=()):
        qq, pp = rel(q, dq), rel(p, dp)
        st, base = slots(qq, pp), owner(c, qq, pp)

        def step(i, carry):
            v = grad[c, order[0, base + i]] + rcv[st + i].astype(F32)
            for ref in extra:
                v += ref[i].astype(F32)
            store(st, i, v)
            return carry

        lax.fori_loop(0, ny, step, 0, unroll=4)
        return st

    def to_sq(st, i, v):
        sq[st + i] = v.astype(BF16)

    two_away = {PLUS: (0, 2), MINUS: (1, 3)}

    rs_t = {}
    for k in range(2):
        for way in (PLUS, MINUS):
            dp = two_away[way][k]
            rs_d[2, dp].wait_recv()
            st = summed(2, dp, to_sq)
            rs_t[way, k] = send(
                remote(sq.at[pl.ds(st, ny)], tq.at[way, k], out.at[2], rqr.at[way, 4 + k], heavies[way]), 2, ny
            )

    rs_m = {}

    def rs_main(way, dp, extra=()):
        dq = 1 if way == PLUS else 3
        rs_d[dq, dp].wait_recv()
        st = summed(dq, dp, to_sq, extra)
        rs_m[way, dp] = send(
            remote(sq.at[pl.ds(st, ny)], mq.at[way, dp], out.at[2], rqr.at[way, dp], heavies[way]), 2, ny
        )

    rs_main(MINUS, 2)
    rs_main(PLUS, 1)
    rs_main(PLUS, 3)
    rs_main(MINUS, 0)

    lane = lax.broadcasted_iota(jnp.int32, (1, owners), 1)

    def invert(f, row):
        return jnp.where(lane == order[0, f], f, row)

    inv_row[...] = lax.fori_loop(0, owners, invert, jnp.zeros((1, owners), jnp.int32), unroll=8)
    load_inv = pltpu.make_async_copy(inv_row, inv, loc.at[0])
    load_inv.start()

    def total(ref, n):
        return ref.at[pl.ds(0, n)]

    def wait_all(ref, n, sem, to):
        remote(total(ref, n), total(ref, n), out.at[0], sem, to).wait_recv()

    wait_all(snd, ny - 1, ayr.at[0], partner)
    ag_p, ag_q = {}, {}

    def piece(dq, dp):
        return gow.at[c, pl.ds(slots(rel(q, dq), rel(p, dp)), ny)]

    def half_piece(dq, dp, j):
        return gow.at[c, pl.ds(slots(rel(q, dq), rel(p, dp)) + j * half, half)]

    def ag_light(way, dp, j, k):
        ag_p[way, k] = send(
            remote(half_piece(0, dp, j), half_piece(0, dp, j), out.at[3], apr.at[way, k], lights[way]), 3, half
        )

    def ag_heavy(way, dq, dp, k):
        ag_q[way, k] = send(
            remote(piece(dq, dp), piece(dq, dp), out.at[4], aqr.at[way, k], heavies[way]), 4, ny
        )

    def ag_across(dq, dp):
        send(remote(piece(dq, dp), piece(dq, dp), out.at[5], adr.at[0], partner), 5, ny)

    ag_light(PLUS, 0, 0, 0)
    ag_light(MINUS, 0, 1, 1)
    ag_light(PLUS, 0, 1, 1)
    ag_light(MINUS, 0, 0, 0)

    for k in (1, 0):
        rs_t[PLUS, k].wait_recv()
        rs_main(PLUS, two_away[PLUS][k], (tq.at[PLUS, k],))
        rs_t[MINUS, k].wait_recv()
        rs_main(MINUS, two_away[MINUS][k], (tq.at[MINUS, k],))

    def ag_own(dp):
        ag_heavy(PLUS, 0, dp, dp)
        ag_heavy(MINUS, 0, dp, dp)
        ag_across(0, dp)

    ag_own(0)
    ag_p[PLUS, 0].wait_recv()
    ag_light(PLUS, 3, 0, 2)
    ag_p[MINUS, 1].wait_recv()
    ag_light(MINUS, 1, 1, 2)
    ag_p[PLUS, 1].wait_recv()
    ag_own(3)
    ag_p[MINUS, 0].wait_recv()
    ag_own(1)
    ag_p[PLUS, 2].wait_recv()
    ag_p[MINUS, 2].wait_recv()
    ag_own(2)

    def heavy_sum(dp):
        rs_d[0, dp].wait_recv()
        rs_m[PLUS, dp].wait_recv()
        rs_m[MINUS, dp].wait_recv()

        def store(st, i, v):
            r1[dp, i] = v

        summed(0, dp, store, (mq.at[PLUS, dp], mq.at[MINUS, dp]))

    rs_pt, rs_pm = {}, {}

    def light_send(way, dp, j, dst, k, table, extra=None):
        def step(i, carry):
            v = r1[dp, j * half + i]
            if extra is not None:
                v += extra[i].astype(F32)
            sp[dp, j * half + i] = v.astype(BF16)
            return carry

        lax.fori_loop(0, half, step, 0, unroll=True)
        table[way, j] = send(
            remote(sp.at[dp, pl.ds(j * half, half)], dst, out.at[6], rpr.at[way, k], lights[way]), 6, half
        )

    heavy_sum(2)
    light_send(PLUS, 2, 0, tp.at[PLUS], 2, rs_pt)
    light_send(MINUS, 2, 1, tp.at[MINUS], 2, rs_pt)
    heavy_sum(1)
    light_send(PLUS, 1, 1, mp.at[PLUS, pl.ds(half, half)], 1, rs_pm)
    heavy_sum(3)
    light_send(MINUS, 3, 0, mp.at[MINUS, pl.ds(0, half)], 0, rs_pm)
    heavy_sum(0)

    forwards = {PLUS: (0, 1), MINUS: (3, 2)}

    def ag_arrived(way, dp):
        ag_q[way, dp].wait_recv()
        dq = 3 if way == PLUS else 1
        if dp in forwards[way]:
            ag_heavy(way, dq, dp, 4 + forwards[way].index(dp))
        ag_across(dq, dp)

    ag_arrived(PLUS, 0)
    ag_arrived(MINUS, 0)
    ag_arrived(PLUS, 3)
    ag_arrived(MINUS, 3)

    rs_pt[PLUS, 0].wait_recv()
    light_send(PLUS, 1, 0, mp.at[PLUS, pl.ds(0, half)], 0, rs_pm, tp.at[PLUS])
    rs_pt[MINUS, 1].wait_recv()
    light_send(MINUS, 3, 1, mp.at[MINUS, pl.ds(half, half)], 1, rs_pm, tp.at[MINUS])

    ag_arrived(PLUS, 1)
    ag_arrived(MINUS, 1)
    ag_arrived(PLUS, 2)
    ag_arrived(MINUS, 2)

    for copy in rs_pm.values():
        copy.wait_recv()

    def light_sum(i, carry):
        v = r1[0, i] + mp[PLUS, i].astype(F32) + mp[MINUS, i].astype(F32)
        r2[i] = v
        sy[i] = v.astype(BF16)
        return carry

    lax.fori_loop(0, ny, light_sum, 0, unroll=4)
    rs_y = [
        send(remote(sy.at[lax.rem(y + d + 1, ny)], yb.at[d], out.at[7], ryr.at[0], y_peers[d]), 7, 1)
        for d in range(ny - 1)
    ]

    for way in (PLUS, MINUS):
        for k in range(2):
            ag_q[way, 4 + k].wait_recv()
            ag_across(2, forwards[way][k])

    wait_all(yb, ny - 1, ryr.at[0], partner)
    value = r2[y]
    for d in range(ny - 1):
        value += yb[d].astype(F32)
    rounded = value.astype(BF16)
    sh[...] = rounded
    hb[h] = rounded
    rs_h = [send(remote(sh, hb.at[h], out.at[8], rhr.at[0], h_peers[d]), 8, 1) for d in range(nh - 1)]

    load_inv.wait()
    remote(gow.at[c], gow.at[1 - c], out.at[0], adr.at[0], partner).wait_recv()

    kacc[...] = jnp.zeros_like(kacc)
    contract = (((1,), (1,)), ((), ()))

    def product(i, carry):
        at = pl.ds(pl.multiple_of(i * CHUNK, CHUNK), CHUNK)
        fs = [inv[0, i * blocks_in_chunk + b] for b in range(blocks_in_chunk)]
        swapped = [lax.rem(f, ny) + (lax.rem(lax.div(f, ny), 4) * 4 + lax.div(f, 4 * ny)) * ny for f in fs]
        w0 = jnp.concatenate([gow[0, f] for f in fs], axis=0)
        w1 = jnp.concatenate([gow[1, f] for f in swapped], axis=0)
        n = nv[:, at]
        kacc[0] += jnp.dot(n, w0, preferred_element_type=F32)
        kacc[1] += jnp.dot(n, w1, preferred_element_type=F32)
        g = lax.dot_general(cv[:, :hw], w0, contract, preferred_element_type=F32)
        g += lax.dot_general(cv[:, hw:], w1, contract, preferred_element_type=F32)
        ig_out[:, at] = g.astype(BF16)
        return carry

    lax.fori_loop(0, chunks, product, 0)
    key_out[:, :hw] = kacc[0].astype(BF16)
    key_out[:, hw:] = kacc[1].astype(BF16)

    if nh > 1:
        wait_all(hb, nh - 1, rhr.at[0], partner)
    for copy in load_m:
        copy.wait()
    value = hb[0].astype(F32)
    for k in range(1, nh):
        value += hb[k].astype(F32)
    fb[c] = mv[c] + value * scale
    last = send(remote(fb.at[c], fb.at[c], out.at[9], fin.at[0], partner), 9, 1)
    last.wait_recv()
    gb_out[:, :hw] = fb[0]
    gb_out[:, hw:] = fb[1]
    sizes = {}
    for group, size in sent:
        sizes[group] = sizes.get(group, 0) + size
    for group, size in sizes.items():
        ref = total(fb if group == 9 else snd, size)
        remote(ref, ref, out.at[group], fin.at[0], partner).wait_send()


def store(ig, key, gb, ig_out, key_out, gb_out, sems):
    micro, tok, width = ig_out.shape
    copies = [pltpu.make_async_copy(gb, gb_out, sems.at[2 * micro])]
    for m in range(micro):
        copies.append(pltpu.make_async_copy(ig.at[pl.ds(m * tok, tok)], ig_out.at[m], sems.at[m]))
        copies.append(pltpu.make_async_copy(key.at[pl.ds(m * tok, tok)], key_out.at[m], sems.at[micro + m]))
    for copy in copies:
        copy.start()
    for copy in copies:
        copy.wait()


def body(ny, nh, normed, kv_cotangent, kv_weight, main_grad, owner_order):
    micro, tok, width = normed.shape
    rows, key_width = kv_weight.shape
    owners = 16 * ny
    hw = key_width // 2
    half = ny // 2
    everyone = owners * nh * 2
    scale = 1.0 / math.sqrt(micro * tok * everyone)
    dma = pltpu.SemaphoreType.DMA
    anywhere = pl.BlockSpec(memory_space=pl.ANY)
    vmem = pl.BlockSpec(memory_space=pltpu.VMEM)
    block = (rows, hw)
    all_rows = micro * tok
    key, ig, gb = pl.pallas_call(
        functools.partial(kernel, ny, nh, scale),
        out_shape=(
            pltpu.VMEM((all_rows, key_width), BF16),
            pltpu.VMEM((all_rows, width), BF16),
            pltpu.VMEM((rows, key_width), F32),
        ),
        in_specs=[anywhere] * 5,
        out_specs=(vmem,) * 3,
        scratch_shapes=[
            pltpu.SMEM((1, owners), jnp.int32),
            pltpu.SMEM((1, owners), jnp.int32),
            pltpu.VMEM((1, owners), jnp.int32),
            pltpu.VMEM((all_rows, width), BF16),
            pltpu.VMEM((all_rows, key_width), BF16),
            pltpu.VMEM((2, *block), F32),
            pltpu.VMEM((2, owners, *block), F32),
            pltpu.VMEM((2, owners, *block), BF16),
            pltpu.VMEM((2, all_rows, hw), F32),
            pltpu.VMEM((owners, *block), BF16),
            pltpu.VMEM((owners, *block), BF16),
            pltpu.VMEM((owners, *block), BF16),
            pltpu.VMEM((2, 2, ny, *block), BF16),
            pltpu.VMEM((2, 4, ny, *block), BF16),
            pltpu.VMEM((4, ny, *block), F32),
            pltpu.VMEM((4, ny, *block), BF16),
            pltpu.VMEM((2, half, *block), BF16),
            pltpu.VMEM((2, ny, *block), BF16),
            pltpu.VMEM((ny, *block), F32),
            pltpu.VMEM((ny, *block), BF16),
            pltpu.VMEM((ny - 1, *block), BF16),
            pltpu.VMEM(block, BF16),
            pltpu.VMEM((nh, *block), BF16),
            pltpu.VMEM((2, *block), F32),
            dma((3 * micro + 4,)),
            dma((10,)),
            dma((1,)),
            dma((2, 3)),
            dma((2, 6)),
            dma((1,)),
            dma((16,)),
            dma((2, 6)),
            dma((2, 3)),
            dma((1,)),
            dma((1,)),
            dma((1,)),
        ],
        compiler_params=pltpu.CompilerParams(
            collective_id=0, has_side_effects=True, vmem_limit_bytes=56 * 1024 * 1024
        ),
    )(owner_order.reshape(1, owners), normed, kv_cotangent, kv_weight, main_grad)
    ig, key, gb = pl.pallas_call(
        store,
        out_shape=(
            jax.ShapeDtypeStruct((micro, tok, width), BF16),
            jax.ShapeDtypeStruct((micro, tok, key_width), BF16),
            jax.ShapeDtypeStruct((rows, key_width), F32),
        ),
        in_specs=[anywhere] * 3,
        out_specs=(anywhere,) * 3,
        scratch_shapes=[dma((2 * micro + 1,))],
        compiler_params=pltpu.CompilerParams(vmem_limit_bytes=1024 * 1024),
    )(ig, key, gb)
    return key, ig, gb


def solution(mesh):
    owners = mesh.shape["fsdp"]
    ny, nh = owners // 16, mesh.shape["dp"] // 2
    split = Mesh(mesh.devices.reshape(4, 4, ny, nh, 2), NAMES)
    tokens, fsdp = P(None, NAMES, None), P(NAMES[:3], None)
    return jax.shard_map(
        functools.partial(body, ny, nh),
        mesh=split,
        in_specs=(tokens, tokens, fsdp, fsdp, P()),
        out_specs=(tokens, tokens, fsdp),
        check_vma=False,
    )
```

time: 66.7 us -> 59.2 us (0.89)
  local copies, waits for them, and re-layouts: 5.46 us -> 0 us
  other arithmetic: 1.28 us -> 0 us
  Pallas kernels: 59.1 us -> 58.4 us
    unnamed x5 -> x0, local copies, waits for them, and re-layouts: 5.46 us -> none
    reduce_sum x1 -> x0, other arithmetic: 1.28 us -> none  [body(): jnp.sum(jnp.where(owner_order[None, :] == indices[:, None], indices[None,...]
    pallas_call x1 -> x2, Pallas kernels: 59.1 us -> 58.4 us  [the longest x1 57 us: body(): pl.pallas_call(functools.partial(kernel, ny, nh, scale), out_shape=(pltpu...]
where the time goes in v2:
time: 59.2 us; the launch traced here: 59.1 us
  Pallas kernels  58.4 us (99%)
  between operations  0.64 us (1%)
    pallas_call x1, Pallas kernels, body(): pl.pallas_call(functools.partial(kernel, ny, nh, scale), out_shape=(pltpu...  57 us
    pallas_call x1, Pallas kernels, body(): pl.pallas_call(store, out_shape=(jax.ShapeDtypeStruct((micro, tok, width)...  1.45 us

profile of v2, /device:TPU:1, one launch (start us, length us, event | category | flops | bytes accessed | tf_op | source)
XLA Modules:
  0.0 59.1 jit_solution(2889825795051427469)
XLA Ops:
  0.6 57.0 %shard_map.76 = (bf16[256,512]{1,0:T(8,128)(2,1)S(1)}, bf16[256,4096]{1,0:T(8,128)(2,1)S(1)}, f32[32,512]{1,0:T(8,128)S(1)}) custom-call(s32[1,128]{1,0:T(1,128)} %bitcast.1, bf16[2,128,4096]{2,1,0:T(8,128)(2,1)} %normed.1, bf16[2,128,512]{2,1,0:T(8,128)(2,1)} %cot.1, bf16[32,512]{1,0:T(8,128)(2,1)} %weight.1, f32[32,512]{1,0:T(8,128)} %main.1), custom_call_target="tpu_custom_call" | custom-call | tf_op jit(solution)/shard_map/pallas_call | solution.py:417
  57.6 1.5 %shard_map.77 = (bf16[2,128,4096]{2,1,0:T(8,128)(2,1)}, bf16[2,128,512]{2,1,0:T(8,128)(2,1)}, f32[32,512]{1,0:T(8,128)}) custom-call(bf16[256,4096]{1,0:T(8,128)(2,1)S(1)} %get-tuple-element.9.ig, bf16[256,512]{1,0:T(8,128)(2,1)S(1)} %get-tuple-element.10.key, f32[32,512]{1,0:T(8,128)S(1)} %get-tuple-element.11.gb), custom_call_target="tpu_custom_call" | custom-call | tf_op jit(solution)/shard_map/pallas_call | solution.py:468

commit v3 on v2

v3 whole, which is shorter than its diff:
```python
import functools
import math

import jax
import jax.numpy as jnp
from jax import lax
from jax.experimental import pallas as pl
from jax.experimental.pallas import tpu as pltpu
from jax.sharding import Mesh
from jax.sharding import PartitionSpec as P

MESH = pl.DeviceIdType.MESH
NAMES = ("zl", "x", "y", "zh", "core")
F32, BF16 = jnp.float32, jnp.bfloat16
CHUNK = 512
PLUS, MINUS = 0, 1
UNITS = ((3, 4), (5, 6), (2, 1), (7, 0))


def kernel(
    ny, nh, scale,
    order_in, normed, cot, weight, main, key_out, ig_out, gb_out,
    order, inv, inv_row, nv, cv, mv, turned, gow, kacc,
    snd, rcv, sq, tq, mq, sy, ty, hy, my, r2, pb, sh, hb, fb,
    loc, out, apr, ayr, aqr, adr, rdr, rqr, ryr, rpr, rhr, fin,
):
    micro, tok, width = normed.shape
    owners, rows, hw = gow.shape[1:]
    blocks_in_chunk = CHUNK // rows
    a, x, y = lax.axis_index("zl"), lax.axis_index("x"), lax.axis_index("y")
    h, c = lax.axis_index("zh"), lax.axis_index("core")
    nz = 4 * nh
    z = h * 4 + a

    def z_of(d):
        to = lax.rem(z + d + nz, nz)
        return lax.rem(to, 4), lax.div(to, 4)

    def heavy(d):
        az, hz = z_of(d)
        xx = lax.rem(x + d + 4, 4)
        return (a + (1 - c) * (az - a), x + c * (xx - x), y, h + (1 - c) * (hz - h), c)

    def light(d):
        az, hz = z_of(d)
        xx = lax.rem(x + d + 4, 4)
        return (a + c * (az - a), x + (1 - c) * (xx - x), y, h + c * (hz - h), c)

    def along(d):
        return (a, x, lax.rem(y + d + ny, ny), h, c)

    q = a + c * (x - a)
    p = x + c * (a - x)
    partner = (a, x, y, h, 1 - c)
    heavies = (heavy(1), heavy(-1))
    lights = (light(1), light(-1), light(2))
    aheads = {d: along(d) for d in (1, -1, 2, -2)}
    h_peers = [(a, x, y, lax.rem(h + d, nh), c) for d in range(1, nh)]
    peers = [partner, *heavies, *lights, light(-2), *aheads.values(), *h_peers]

    def rel(v, d):
        return lax.rem(v + d, 4)

    def yrel(d):
        return lax.rem(y + d + ny, ny)

    def owner(cc, qq, yy, pp):
        return ((qq + cc * (pp - qq)) * 4 + (pp + cc * (qq - pp))) * ny + yy

    def remote(src, dst, s, r, to):
        return pltpu.make_async_remote_copy(
            src_ref=src, dst_ref=dst, send_sem=s, recv_sem=r, device_id=to, device_id_type=MESH
        )

    mine = (q * ny + y) * 4 + p
    load_w = pltpu.make_async_copy(
        weight.at[:, pl.ds(pl.multiple_of(c * hw, hw), hw)], gow.at[c, mine], loc.at[0]
    )
    load_order = pltpu.make_async_copy(order_in, order, loc.at[1])
    loads = [
        pltpu.make_async_copy(
            cot.at[m, :, pl.ds(k * hw, hw)], cv.at[k, pl.ds(m * tok, tok)], loc.at[2 + 2 * m + k]
        )
        for m in range(micro)
        for k in range(2)
    ]
    loads.append(load_order)
    wide = width // 2
    wides = [
        [
            pltpu.make_async_copy(
                normed.at[m, :, pl.ds(k * wide, wide)],
                nv.at[pl.ds(m * tok, tok), pl.ds(k * wide, wide)],
                loc.at[2 + (2 + k) * micro + m],
            )
            for m in range(micro)
        ]
        for k in range(2)
    ]
    load_m = [
        pltpu.make_async_copy(main.at[:, pl.ds(k * hw, hw)], mv.at[k], loc.at[2 + 4 * micro + k]) for k in range(2)
    ]
    load_w.start()
    for copy in wides[0] + wides[1] + loads + load_m:
        copy.start()

    barrier = pltpu.get_barrier_semaphore()
    for peer in peers:
        pl.semaphore_signal(barrier, inc=1, device_id=peer, device_id_type=MESH)

    chunks = width // CHUNK
    sent = []

    def send(copy, group, size):
        copy.start()
        sent.append((group, size))
        return copy

    def turn(i, carry):
        at = pl.multiple_of(i * CHUNK, CHUNK)
        block = nv[:, pl.ds(at, CHUNK)].T
        turned[pl.ds(i * blocks_in_chunk, blocks_in_chunk)] = block.reshape(blocks_in_chunk, rows, micro * tok)
        return carry

    def gradient(cc, qq, u):
        which = [owner(cc, qq, yrel(d), pp) for d in UNITS[u] for pp in range(4)]
        block = jnp.concatenate([turned[order[0, f]] for f in which], axis=0)
        return jnp.dot(block, cv[cc], preferred_element_type=F32).reshape(8, rows, hw)

    def unit(qq, u):
        return pl.ds((qq * 4 + u) * 8, 8)

    def prepare():
        for k in range(2):
            for copy in wides[k]:
                copy.wait()
            lax.fori_loop(k * chunks // 2, (k + 1) * chunks // 2, turn, 0, unroll=2)
        for copy in loads:
            copy.wait()

    def partners(dq, u):
        qq = rel(p, dq)
        snd[unit(qq, u)] = gradient(1 - c, qq, u).astype(BF16)

    far = jnp.minimum(y, ny - y) // max(ny // 2 - 1, 1) * (h // max(nh - 1, 1))
    late = far > 0
    early = far == 0

    @pl.when(early)
    def _():
        prepare()
        for dq in (2, 1, 3, 0):
            for u in range(4):
                partners(dq, u)

    load_w.wait()
    pl.semaphore_wait(barrier, len(peers))
    own = gow.at[c, mine]
    ag_p = [send(remote(own, own, out.at[0], apr.at[k], lights[k]), 0, 1) for k in range(3)]

    pl.when(late)(prepare)

    rs_d = {}

    def give(dq):
        @pl.when(late)
        def _():
            for u in range(4):
                partners(dq, u)

        for u in range(4):
            ref = unit(rel(p, dq), u)
            rs_d[dq, u] = send(
                remote(snd.at[ref], rcv.at[ref], out.at[1], rdr.at[dq * 4 + u], partner), 1, 8
            )

    def summed(dq, u, extra=()):
        qq = rel(q, dq)
        v = gradient(c, qq, u) + rcv[unit(qq, u)].astype(F32)
        for ref in extra:
            v += ref[...].astype(F32)
        return v

    def to_sq(dq, u, extra=()):
        ref = unit(rel(q, dq), u)
        sq[ref] = summed(dq, u, extra).astype(BF16)
        return sq.at[ref]

    two_away = {PLUS: (0, 2), MINUS: (1, 3)}

    give(2)
    give(1)

    rs_t = {}
    for k in range(2):
        for way in (PLUS, MINUS):
            u = two_away[way][k]
            rs_d[2, u].wait_recv()
            rs_t[way, k] = send(
                remote(to_sq(2, u), tq.at[way, k], out.at[2], rqr.at[way, 4 + k], heavies[way]), 2, 8
            )

    give(3)

    for copy in ag_p:
        copy.wait_recv()

    def piece(dq, d):
        return gow.at[c, pl.ds((rel(q, dq) * ny + yrel(d)) * 4, 4)]

    def half_piece(d, j):
        return gow.at[c, pl.ds((q * ny + yrel(d)) * 4 + 2 * j, 2)]

    ag_y, ag_q = {}, {}

    def ag_along(k, d, ref, size):
        ag_y[k] = send(remote(ref, ref, out.at[3], ayr.at[k], aheads[d]), 3, size)

    def ag_heavy(way, dq, d, k):
        ref = piece(dq, d)
        ag_q[way, k] = send(remote(ref, ref, out.at[4], aqr.at[way, k], heavies[way]), 4, 4)

    def ag_across(dq, d):
        ref = piece(dq, d)
        send(remote(ref, ref, out.at[5], adr.at[0], partner), 5, 4)

    def ag_own(d):
        ag_heavy(PLUS, 0, d, d)
        ag_heavy(MINUS, 0, d, d)
        ag_across(0, d)

    ag_along(0, 2, piece(0, 0), 4)
    ag_along(1, -2, piece(0, 0), 4)
    ag_along(2, 1, piece(0, 0), 4)
    ag_along(3, -1, piece(0, 0), 4)

    give(0)

    rs_m = {}

    def rs_main(way, u, extra=()):
        dq = 1 if way == PLUS else 3
        rs_d[dq, u].wait_recv()
        rs_m[way, u] = send(
            remote(to_sq(dq, u, extra), mq.at[way, u], out.at[2], rqr.at[way, u], heavies[way]), 2, 8
        )

    rs_main(PLUS, 1)
    rs_main(MINUS, 0)
    rs_main(PLUS, 3)
    rs_main(MINUS, 2)

    lane = lax.broadcasted_iota(jnp.int32, (1, owners), 1)

    def invert(f, row):
        return jnp.where(lane == order[0, f], f, row)

    inv_row[...] = lax.fori_loop(0, owners, invert, jnp.zeros((1, owners), jnp.int32), unroll=8)
    load_inv = pltpu.make_async_copy(inv_row, inv, loc.at[0])
    load_inv.start()

    def carry(k):
        for way in (PLUS, MINUS):
            rs_t[way, k].wait_recv()
            rs_main(way, two_away[way][k], (tq.at[way, k],))

    carry(0)
    carry(1)
    ag_own(0)
    ag_y[0].wait_recv()
    ag_along(4, 1, piece(0, -2), 4)
    ag_along(6, 2, half_piece(-2, 0), 2)
    ag_y[1].wait_recv()
    ag_along(5, -1, piece(0, 2), 4)
    ag_along(7, -2, half_piece(2, 1), 2)
    ag_y[2].wait_recv()
    ag_own(7)
    ag_y[3].wait_recv()
    ag_own(1)
    ag_own(6)
    ag_own(2)

    def heavy_sum(u):
        rs_d[0, u].wait_recv()
        rs_m[PLUS, u].wait_recv()
        rs_m[MINUS, u].wait_recv()
        return summed(0, u, (mq.at[PLUS, u], mq.at[MINUS, u]))

    rs_y = {}

    def y_send(k, d, src, dst, size):
        rs_y[k] = send(remote(src, dst, out.at[6], ryr.at[k], aheads[d]), 6, size)

    sy[0] = heavy_sum(0).astype(BF16)
    y_send(0, 1, sy.at[0, pl.ds(0, 4)], ty.at[0], 4)
    y_send(2, 2, sy.at[0, pl.ds(4, 2)], hy.at[0], 2)
    y_send(3, -2, sy.at[0, pl.ds(6, 2)], hy.at[1], 2)
    v = heavy_sum(1)
    sy[1, pl.ds(0, 4)] = v[:4].astype(BF16)
    y_send(1, -1, sy.at[1, pl.ds(0, 4)], ty.at[1], 4)
    r2[1] = v[4:]
    v = heavy_sum(2)
    r2[2] = v[:4]
    sy[2, pl.ds(4, 4)] = v[4:].astype(BF16)
    y_send(4, 1, sy.at[2, pl.ds(4, 4)], my.at[0], 4)
    v = heavy_sum(3)
    sy[3, pl.ds(0, 4)] = v[:4].astype(BF16)
    y_send(5, -1, sy.at[3, pl.ds(0, 4)], my.at[1], 4)
    r2[0] = v[4:]

    forwards = {PLUS: (0, 1, 6, 3), MINUS: (7, 2, 5, 4)}

    def ag_arrived(d):
        for way in (PLUS, MINUS):
            ag_q[way, d].wait_recv()
            dq = 3 if way == PLUS else 1
            if d in forwards[way]:
                ag_heavy(way, dq, d, 8 + forwards[way].index(d))
            ag_across(dq, d)

    ag_arrived(0)
    ag_y[4].wait_recv()
    ag_own(5)
    ag_y[5].wait_recv()
    ag_own(3)
    ag_y[6].wait_recv()
    ag_y[7].wait_recv()
    ag_own(4)

    ag_arrived(7)
    ag_arrived(1)
    rs_y[0].wait_recv()
    rs_y[2].wait_recv()
    sy[2, pl.ds(0, 2)] = (r2[2, :2] + ty[0, :2].astype(F32) + hy[0].astype(F32)).astype(BF16)
    sy[2, pl.ds(2, 2)] = (r2[2, 2:] + ty[0, 2:].astype(F32)).astype(BF16)
    y_send(6, 2, sy.at[2, pl.ds(0, 4)], my.at[2], 4)
    rs_y[1].wait_recv()
    rs_y[3].wait_recv()
    sy[1, pl.ds(4, 2)] = (r2[1, :2] + ty[1, :2].astype(F32)).astype(BF16)
    sy[1, pl.ds(6, 2)] = (r2[1, 2:] + ty[1, 2:].astype(F32) + hy[1].astype(F32)).astype(BF16)
    y_send(7, -2, sy.at[1, pl.ds(4, 4)], my.at[3], 4)

    for d in (6, 2, 5, 3, 4):
        ag_arrived(d)
    for k in (4, 5, 6, 7):
        rs_y[k].wait_recv()
    v = r2[0]
    for k in range(4):
        v += my[k].astype(F32)
    r2[0] = v
    sy[3, pl.ds(4, 4)] = v.astype(BF16)
    rs_p = [
        send(remote(sy.at[3, 4 + rel(p, d)], pb.at[k], out.at[7], rpr.at[k], lights[k]), 7, 1)
        for k, d in enumerate((1, 3, 2))
    ]

    for k in range(4):
        for way in (PLUS, MINUS):
            ag_q[way, 8 + k].wait_recv()
            ag_across(2, forwards[way][k])

    for copy in rs_p:
        copy.wait_recv()
    value = r2[0, p]
    for k in range(3):
        value += pb[k].astype(F32)
    rounded = value.astype(BF16)
    sh[...] = rounded
    hb[h] = rounded
    rs_h = [send(remote(sh, hb.at[h], out.at[8], rhr.at[0], h_peers[d]), 8, 1) for d in range(nh - 1)]

    load_inv.wait()
    remote(gow.at[c], gow.at[1 - c], out.at[0], adr.at[0], partner).wait_recv()

    kacc[...] = jnp.zeros_like(kacc)
    contract = (((1,), (1,)), ((), ()))

    def product(i, carry):
        at = pl.ds(pl.multiple_of(i * CHUNK, CHUNK), CHUNK)
        fs = [inv[0, i * blocks_in_chunk + b] for b in range(blocks_in_chunk)]
        parts = [(lax.div(f, 4 * ny), lax.rem(lax.div(f, ny), 4), lax.rem(f, ny)) for f in fs]
        w0 = jnp.concatenate([gow[0, (fz * ny + fy) * 4 + fx] for fz, fx, fy in parts], axis=0)
        w1 = jnp.concatenate([gow[1, (fx * ny + fy) * 4 + fz] for fz, fx, fy in parts], axis=0)
        n = nv[:, at]
        kacc[0] += jnp.dot(n, w0, preferred_element_type=F32)
        kacc[1] += jnp.dot(n, w1, preferred_element_type=F32)
        g = lax.dot_general(cv[0], w0, contract, preferred_element_type=F32)
        g += lax.dot_general(cv[1], w1, contract, preferred_element_type=F32)
        ig_out[:, at] = g.astype(BF16)
        return carry

    lax.fori_loop(0, chunks, product, 0)
    key_out[:, :hw] = kacc[0].astype(BF16)
    key_out[:, hw:] = kacc[1].astype(BF16)

    def total(ref, n):
        return ref.at[pl.ds(0, n)]

    if nh > 1:
        ref = total(hb, nh - 1)
        remote(ref, ref, out.at[0], rhr.at[0], partner).wait_recv()
    for copy in load_m:
        copy.wait()
    value = hb[0].astype(F32)
    for k in range(1, nh):
        value += hb[k].astype(F32)
    fb[c] = mv[c] + value * scale
    last = send(remote(fb.at[c], fb.at[c], out.at[9], fin.at[0], partner), 9, 1)
    last.wait_recv()
    gb_out[:, :hw] = fb[0]
    gb_out[:, hw:] = fb[1]
    sizes = {}
    for group, size in sent:
        sizes[group] = sizes.get(group, 0) + size
    for group, size in sizes.items():
        ref = total(fb if group == 9 else snd, size)
        remote(ref, ref, out.at[group], fin.at[0], partner).wait_send()


def store(ig, key, gb, ig_out, key_out, gb_out, sems):
    micro, tok, width = ig_out.shape
    copies = [pltpu.make_async_copy(gb, gb_out, sems.at[2 * micro])]
    for m in range(micro):
        copies.append(pltpu.make_async_copy(ig.at[pl.ds(m * tok, tok)], ig_out.at[m], sems.at[m]))
        copies.append(pltpu.make_async_copy(key.at[pl.ds(m * tok, tok)], key_out.at[m], sems.at[micro + m]))
    for copy in copies:
        copy.start()
    for copy in copies:
        copy.wait()


def body(ny, nh, normed, kv_cotangent, kv_weight, main_grad, owner_order):
    micro, tok, width = normed.shape
    rows, key_width = kv_weight.shape
    owners = 16 * ny
    hw = key_width // 2
    everyone = owners * nh * 2
    scale = 1.0 / math.sqrt(micro * tok * everyone)
    dma = pltpu.SemaphoreType.DMA
    anywhere = pl.BlockSpec(memory_space=pl.ANY)
    vmem = pl.BlockSpec(memory_space=pltpu.VMEM)
    block = (rows, hw)
    all_rows = micro * tok
    key, ig, gb = pl.pallas_call(
        functools.partial(kernel, ny, nh, scale),
        out_shape=(
            pltpu.VMEM((all_rows, key_width), BF16),
            pltpu.VMEM((all_rows, width), BF16),
            pltpu.VMEM((rows, key_width), F32),
        ),
        in_specs=[anywhere] * 5,
        out_specs=(vmem,) * 3,
        scratch_shapes=[
            pltpu.SMEM((1, owners), jnp.int32),
            pltpu.SMEM((1, owners), jnp.int32),
            pltpu.VMEM((1, owners), jnp.int32),
            pltpu.VMEM((all_rows, width), BF16),
            pltpu.VMEM((2, all_rows, hw), BF16),
            pltpu.VMEM((2, *block), F32),
            pltpu.VMEM((owners, rows, all_rows), BF16),
            pltpu.VMEM((2, owners, *block), BF16),
            pltpu.VMEM((2, all_rows, hw), F32),
            pltpu.VMEM((owners, *block), BF16),
            pltpu.VMEM((owners, *block), BF16),
            pltpu.VMEM((owners, *block), BF16),
            pltpu.VMEM((2, 2, 8, *block), BF16),
            pltpu.VMEM((2, 4, 8, *block), BF16),
            pltpu.VMEM((4, 8, *block), BF16),
            pltpu.VMEM((2, 4, *block), BF16),
            pltpu.VMEM((2, 2, *block), BF16),
            pltpu.VMEM((4, 4, *block), BF16),
            pltpu.VMEM((3, 4, *block), F32),
            pltpu.VMEM((3, *block), BF16),
            pltpu.VMEM(block, BF16),
            pltpu.VMEM((nh, *block), BF16),
            pltpu.VMEM((2, *block), F32),
            dma((4 * micro + 4,)),
            dma((10,)),
            dma((3,)),
            dma((8,)),
            dma((2, 12)),
            dma((1,)),
            dma((16,)),
            dma((2, 6)),
            dma((8,)),
            dma((3,)),
            dma((1,)),
            dma((1,)),
        ],
        compiler_params=pltpu.CompilerParams(
            collective_id=0, has_side_effects=True, vmem_limit_bytes=56 * 1024 * 1024
        ),
    )(owner_order.reshape(1, owners), normed, kv_cotangent, kv_weight, main_grad)
    ig, key, gb = pl.pallas_call(
        store,
        out_shape=(
            jax.ShapeDtypeStruct((micro, tok, width), BF16),
            jax.ShapeDtypeStruct((micro, tok, key_width), BF16),
            jax.ShapeDtypeStruct((rows, key_width), F32),
        ),
        in_specs=[anywhere] * 3,
        out_specs=(anywhere,) * 3,
        scratch_shapes=[dma((2 * micro + 1,))],
        compiler_params=pltpu.CompilerParams(vmem_limit_bytes=1024 * 1024),
    )(ig, key, gb)
    return key, ig, gb


def solution(mesh):
    owners = mesh.shape["fsdp"]
    ny, nh = owners // 16, mesh.shape["dp"] // 2
    split = Mesh(mesh.devices.reshape(4, 4, ny, nh, 2), NAMES)
    tokens, fsdp = P(None, NAMES, None), P(NAMES[:3], None)
    return jax.shard_map(
        functools.partial(body, ny, nh),
        mesh=split,
        in_specs=(tokens, tokens, fsdp, fsdp, P()),
        out_specs=(tokens, tokens, fsdp),
        check_vma=False,
    )
```

time: 59.2 us -> 53 us (0.90)
  Pallas kernels: 58.4 us -> 52.2 us
    pallas_call x1, Pallas kernels: 57 us -> 50.8 us  [body(): pl.pallas_call(functools.partial(kernel, ny, nh, scale), out_shape=(pltpu...]
where the time goes in v3:
time: 53 us; the launch traced here: 52.9 us
  Pallas kernels  52.2 us (98%)
  between operations  0.64 us (1%)
    pallas_call x1, Pallas kernels, body(): pl.pallas_call(functools.partial(kernel, ny, nh, scale), out_shape=(pltpu...  50.8 us
    pallas_call x1, Pallas kernels, body(): pl.pallas_call(store, out_shape=(jax.ShapeDtypeStruct((micro, tok, width)...  1.45 us

profile of v3, /device:TPU:1, one launch (start us, length us, event | category | flops | bytes accessed | tf_op | source)
XLA Modules:
  0.0 52.9 jit_solution(11739246700336825477)
XLA Ops:
  0.6 50.8 %shard_map.76 = (bf16[256,512]{1,0:T(8,128)(2,1)S(1)}, bf16[256,4096]{1,0:T(8,128)(2,1)S(1)}, f32[32,512]{1,0:T(8,128)S(1)}) custom-call(s32[1,128]{1,0:T(1,128)} %bitcast.1, bf16[2,128,4096]{2,1,0:T(8,128)(2,1)} %normed.1, bf16[2,128,512]{2,1,0:T(8,128)(2,1)} %cot.1, bf16[32,512]{1,0:T(8,128)(2,1)} %weight.1, f32[32,512]{1,0:T(8,128)} %main.1), custom_call_target="tpu_custom_call" | custom-call | tf_op jit(solution)/shard_map/pallas_call | solution.py:444
  51.4 1.5 %shard_map.77 = (bf16[2,128,4096]{2,1,0:T(8,128)(2,1)}, bf16[2,128,512]{2,1,0:T(8,128)(2,1)}, f32[32,512]{1,0:T(8,128)}) custom-call(bf16[256,4096]{1,0:T(8,128)(2,1)S(1)} %get-tuple-element.9.ig, bf16[256,512]{1,0:T(8,128)(2,1)S(1)} %get-tuple-element.10.key, f32[32,512]{1,0:T(8,128)S(1)} %get-tuple-element.11.gb), custom_call_target="tpu_custom_call" | custom-call | tf_op jit(solution)/shard_map/pallas_call | solution.py:494
